TPU v7x, 32 devices: a whole 2x2x4 slice. The times are simulated.
32 devices in a mesh: cuts: 8 (over z, y), event: 4 (over x, core).
Axes of the slice: x: 2, y: 2, z: 4, core: 2. Of those that a mesh axis runs over, the one named last changes fastest.
Arguments:
- kernels: float32 [4, 64, 128, 256], P('event', 'cuts'), may hold values from -24 to 24
- steps: float32 [8, 64, 128, 256], P(None, 'cuts', 'event'), may hold values from -11 to 11
- curvature: float32 [8, 64, 128, 256], P(None, 'cuts', 'event'), may hold values from 0.2 to 5
Outputs:
- gradient: float32 [64, 128, 256], P('cuts', 'event')
- direction: float32 [64, 128, 256], P('cuts', 'event')
All inputs are finite; a program needn't handle non-finite values.
Results may differ from a plain program's by a relative error of at most 0.00021.
Values sent between devices are 32-bit elements; how exact they have to be, the bound alone decides.
A program may use at most 64 MiB of HBM per device.

v0:
```python
import math
import jax
import jax.numpy as jnp
from jax import lax
from jax.sharding import PartitionSpec as P

PAIRS = 8
RIM = 4


def with_halo(cells, sides, width):
    for axis, dim in sides:
        count = lax.axis_size(axis)
        head = lax.slice_in_dim(cells, 0, width, axis=dim)
        tail = lax.slice_in_dim(cells, cells.shape[dim] - width, cells.shape[dim], axis=dim)
        cells = jnp.concatenate(
            [
                lax.ppermute(tail, axis, [(i, (i + 1) % count) for i in range(count)]),
                cells,
                lax.ppermute(head, axis, [((i + 1) % count, i) for i in range(count)]),
            ],
            axis=dim,
        )
    return cells


def gauss_matrix(length, sigma):
    points = jnp.arange(length, dtype=jnp.float32)
    offset = points[:, None] - points[None, :]
    matrix = jnp.exp(-offset * offset / (2.0 * sigma * sigma))
    return matrix / jnp.sum(matrix, axis=1, keepdims=True)


def cycle_weights():
    unscaled = [math.exp(-((column - RIM) ** 2) / 4.5) for column in range(2 * RIM + 1)]
    whole = sum(unscaled)
    return [weight / whole for weight in unscaled]


def smooth_plane(field):
    lat_len = field.shape[2]
    plane = jnp.dot(
        field.reshape(-1, lat_len), gauss_matrix(lat_len, 4.0).T, precision=lax.Precision.HIGHEST
    ).reshape(field.shape)
    padded = with_halo(plane, (("cuts", 0),), RIM)
    lon_len = plane.shape[0]
    weights = cycle_weights()
    smoothed = jnp.zeros_like(plane)
    for column in range(2 * RIM + 1):
        smoothed = smoothed + weights[column] * padded[column : column + lon_len]
    return smoothed


def shards(kernels, steps, curvature):
    partial_value = kernels[0]
    rad_len = partial_value.shape[1]
    radial = jnp.einsum(
        "ij,ajb->aib", gauss_matrix(rad_len, 3.0), partial_value, precision=lax.Precision.HIGHEST
    )
    summed = lax.psum(radial, "event")
    smoothed = smooth_plane(summed)
    portion = rad_len // lax.axis_size("event")
    gradient = lax.dynamic_slice_in_dim(smoothed, lax.axis_index("event") * portion, portion, 1)
    changes = curvature * steps
    vectors = jnp.concatenate(
        [steps.reshape(PAIRS, -1), changes.reshape(PAIRS, -1), gradient.reshape(1, -1)], axis=0
    )
    products = lax.psum(
        jnp.dot(vectors, vectors.T, precision=lax.Precision.HIGHEST), ("cuts", "event")
    )
    curvs = jnp.diagonal(products[:PAIRS, PAIRS : 2 * PAIRS])
    inverse = 1.0 / curvs
    scaling = curvs[PAIRS - 1] / products[2 * PAIRS - 1, 2 * PAIRS - 1]
    weights_now = jnp.zeros((2 * PAIRS + 1,), jnp.float32).at[2 * PAIRS].set(1.0)
    alphas = [None] * PAIRS
    for pair in reversed(range(PAIRS)):
        alphas[pair] = inverse[pair] * jnp.dot(
            products[pair], weights_now, precision=lax.Precision.HIGHEST
        )
        weights_now = weights_now.at[PAIRS + pair].add(-alphas[pair])
    weights_now = scaling * weights_now
    for pair in range(PAIRS):
        second = inverse[pair] * jnp.dot(
            products[PAIRS + pair], weights_now, precision=lax.Precision.HIGHEST
        )
        weights_now = weights_now.at[pair].add(alphas[pair] - second)
    direction = -jnp.dot(weights_now[None, :], vectors, precision=lax.Precision.HIGHEST).reshape(
        gradient.shape
    )
    return (gradient, direction)


def solution(mesh):
    placed = (
        P("event", "cuts", None, None),
        P(None, "cuts", "event", None),
        P(None, "cuts", "event", None),
    )
    return jax.shard_map(
        shards,
        mesh=mesh,
        in_specs=placed,
        out_specs=(P("cuts", "event", None), P("cuts", "event", None)),
        check_vma=False,
    )
```

profile of v0, /device:TPU:0, one launch (start us, length us, event | category | flops | bytes accessed | tf_op | source)
XLA Modules:
  0.0 200.9 jit_solution(306684947524946787)
XLA Ops:
  7.4 1.0 copy-done
  8.4 2.0 %fusion.11 = f32[128,8,256]{2,0,1:T(8,128)} fusion(f32[1,8,128,256]{3,2,1,0:T(8,128)S(1)} %copy-done, f32[128]{0:T(128)S(1)} %fusion.36), kind=kOutput, calls=%fused_computation.27 | convolution fusion | flops 402735104 | bytes 2097664 | tf_op jit(solution)/shard_map/ij,ajb->aib/dot_general | solution.py:57
  10.5 1.2 copy.40
  11.7 1.5 constant_dynamic-update-slice_fusion.1
  13.2 0.4 mul.113
  13.6 2.6 %copy.41 = f32[1,8,256,256]{3,1,2,0:T(8,128)} copy(f32[1,8,256,256]{3,2,1,0:T(8,128)S(1)} %bitcast.165) | data formatting | bytes 4194304
  16.2 0.2 fusion.28
  16.4 33.3 %all-reduce.2.cloned.1.call-done = f32[1024,256]{1,0:T(8,128)} async-done(((f32[1024,256]{1,0:T(8,128)}), f32[1024,256]{1,0:T(8,128)}) %all-reduce.2.cloned.1.call-update) | async-done | bytes 1048592 | tf_op jit(solution)/shard_map/psum | solution.py:60
  49.6 2.5 %fusion.25 = f32[1024,256]{1,0:T(8,128)S(1)} fusion(f32[1024,256]{1,0:T(8,128)} %all-reduce.2.cloned.1.call-done, f32[256]{0:T(256)S(1)} %fusion.28), kind=kOutput, calls=%fused_computation.48 | convolution fusion | flops 805634048 | bytes 2098176 | tf_op jit(solution)/shard_map/dot_general | solution.py:42
  52.1 0.9 fusion.74
  53.0 1.5 collective-permute-start
  54.5 3.2 %collective-permute-start.1 = (f32[4,128,256]{2,1,0:T(8,128)}, f32[4,128,256]{2,1,0:T(8,128)S(1)}, u32[]{:S(2)}, u32[]{:S(2)}) collective-permute-start(f32[4,128,256]{2,1,0:T(8,128)} %bitcast.6), channel_id=1, source_target_pairs={{4,0},{8,4},{12,8},{16,12},{20,16},{24,20},{28,24},{0,28},{5,1},{9... | collective-permute-start | bytes 1572872 | tf_op jit(solution)/shard_map/ppermute | solution.py:20
  57.7 1.4 constant_dynamic-update-slice_fusion
  59.2 19.6 %collective-permute-done.1 = f32[4,128,256]{2,1,0:T(8,128)S(1)} collective-permute-done((f32[4,128,256]{2,1,0:T(8,128)}, f32[4,128,256]{2,1,0:T(8,128)S(1)}, u32[]{:S(2)}, u32[]{:S(2)}) %collective-permute-start.1) | collective-permute-done | bytes 524320 | tf_op jit(solution)/shard_map/ppermute | solution.py:20
  78.7 0.3 pad_slice_fusion.4
  79.1 2.1 %fusion.4 = (f32[8,128,256]{2,1,0:T(8,128)S(1)}, f32[8,128,256]{2,1,0:T(8,128)S(1)}, f32[8,128,256]{2,1,0:T(8,128)S(1)}, f32[8,128,256]{2,1,0:T(8,128)S(1)}, f32[8,128,256]{2,1,0:T(8,128)S(1)}) fusion(f32[8,128,256]{2,1,0:T(8,128)S(1)} %bitcast.161, f32[4,128,256]{2,1,0:T(8,128)} %collective-permute-done), kind=kLoop, calls=%fused_computation.17 | loop fusion | flops 2621440 | bytes 6815744 | tf_op jit(solution)/shard_map/add | solution.py:50
  81.2 0.2 fusion.17
  81.4 0.3 reshape.412
  81.7 6.0 %dynamic-update-slice.38 = f32[17,65536]{1,0:T(8,128)} dynamic-update-slice(f32[17,65536]{1,0:T(8,128)} %constant_dynamic-update-slice_fusion, f32[1,65536]{1,0:T(1,128)S(1)} %reshape.412, s32[]{} %constant.465, s32[]{} %constant.463) | dynamic-update-slice | bytes 524292 | tf_op jit(solution)/shard_map/concatenate | solution.py:65
  87.7 8.8 %fusion.76 = f32[17,17]{1,0:T(8,128)S(1)} fusion(f32[17,65536]{1,0:T(8,128)} %dynamic-update-slice.38), kind=kOutput, calls=%fused_computation.135 | convolution fusion | flops 227278848 | bytes 4457604 | tf_op jit(solution)/shard_map/dot_general | solution.py:69
  96.5 39.4 %psum.15 = f32[17,17]{1,0:T(8,128)S(1)} all-reduce(f32[17,17]{1,0:T(8,128)S(1)} %fusion.76), channel_id=1, replica_groups=mesh['cuts'=8,'event'=4] {'cuts','event'}, use_global_device_ids=true, to_apply=%region_3.0 | all-reduce | flops 289 | bytes 2312 | tf_op jit(solution)/shard_map/psum | solution.py:68
  136.0 0.6 gather_fusion
  136.6 0.6 slice.344
  137.2 0.6 slice.402
  137.8 0.7 fusion.75
  138.5 0.6 fusion.70
  140.3 1.3 fusion.68
  142.9 0.2 constant_dynamic-update-slice_fusion.14
  143.1 1.3 fusion.66
  145.7 0.2 constant_dynamic-update-slice_fusion.13
  145.8 1.3 fusion.64
  148.4 0.2 constant_dynamic-update-slice_fusion.12
  148.6 1.3 fusion.62
  151.3 1.3 fusion.60
  154.1 1.3 fusion.58
  156.8 1.3 fusion.56
  160.7 1.3 fusion.54
  163.2 1.3 fusion.52
  166.0 1.4 fusion.50
  168.8 1.4 fusion.48
  171.6 1.3 fusion.46
  174.2 1.3 fusion.44
  177.0 1.4 fusion.42
  179.7 1.3 fusion.40
  182.4 4.8 %copy.42 = f32[3,8,256,256]{3,2,1,0:T(8,128)S(1)} copy(f32[3,8,256,256]{3,1,2,0:T(8,128)} %bitcast.159) | data formatting | bytes 12582912
  187.2 0.4 slice.419
  187.7 5.6 %fusion = f32[1,8,32,256]{3,0,2,1:T(1,128)S(1)} fusion(f32[8,32,256,17]{2,1,0,3:T(8,128)S(1)} %bitcast.160, f32[17]{0:T(128)S(1)} %add_dynamic-update-slice_fusion), kind=kOutput, calls=%fused_computation.1 | convolution fusion | flops 13369344 | bytes 4718660 | tf_op jit(solution)/shard_map/dot_general | solution.py:87
  193.3 0.7 bitcast_negate_fusion
  (34 shorter events, 2.0 us)
Async XLA Ops:
  7.2 1.2 copy-start
  7.2 3.3 %copy-start.1 = (f32[8,8,32,256]{3,2,1,0:T(8,128)S(1)}, f32[8,8,32,256]{3,2,1,0:T(8,128)}, u32[]{:S(2)}) copy-start(f32[8,8,32,256]{3,2,1,0:T(8,128)} %param.38) | copy-start | bytes 6291460
  7.2 42.4 %all-reduce.2.cloned.1.call-start = ((), (), s32[]{:S(2)}) async-start(), calls=%async_computation | async-start | bytes 2097152 | tf_op jit(solution)/shard_map/psum | solution.py:60
  10.5 2.7 %copy-start.3 = (f32[8,8,32,256]{3,2,1,0:T(8,128)S(1)}, f32[8,8,32,256]{3,2,1,0:T(8,128)}, u32[]{:S(2)}) copy-start(f32[8,8,32,256]{3,2,1,0:T(8,128)} %param.39) | copy-start | bytes 6291460
  16.2 43.0 %copy-start.6 = (f32[17]{0:T(128)S(1)}, f32[17]{0:T(128)}, u32[]{:S(2)}) copy-start(f32[17]{0:T(128)} %constant.416.clone.1) | copy-start | bytes 208
  49.6 8.1 %copy-start.2 = (f32[1,8,256,256]{3,1,2,0:T(8,128)S(1)}, f32[1,8,256,256]{3,1,2,0:T(8,128)}, u32[]{:S(2)}) copy-start(f32[1,8,256,256]{3,1,2,0:T(8,128)} %copy.41) | copy-start | bytes 6291460
  53.0 26.0 %collective-permute-start = (f32[4,128,256]{2,1,0:T(8,128)S(1)}, f32[4,128,256]{2,1,0:T(8,128)}, u32[]{:S(2)}, u32[]{:S(2)}) collective-permute-start(f32[4,128,256]{2,1,0:T(8,128)S(1)} %bitcast.169), channel_id=1, source_target_pairs={{0,4},{4,8},{8,12},{12,16},{16,20},{20,24},{24,28},{28,0},{1,5},{5... | collective-permute-start | bytes 1572872 | tf_op jit(solution)/shard_map/ppermute | solution.py:18
  54.5 24.2 %collective-permute-start.1 = (f32[4,128,256]{2,1,0:T(8,128)}, f32[4,128,256]{2,1,0:T(8,128)S(1)}, u32[]{:S(2)}, u32[]{:S(2)}) collective-permute-start(f32[4,128,256]{2,1,0:T(8,128)} %bitcast.6), channel_id=1, source_target_pairs={{4,0},{8,4},{12,8},{16,12},{20,16},{24,20},{28,24},{0,28},{5,1},{9... | collective-permute-start | bytes 1572872 | tf_op jit(solution)/shard_map/ppermute | solution.py:20
  81.4 15.1 %copy-start.4 = (f32[8,32,256]{2,1,0:T(8,128)}, f32[8,32,256]{2,1,0:T(8,128)S(1)}, u32[]{:S(2)}) copy-start(f32[8,32,256]{2,1,0:T(8,128)S(1)} %fusion.17) | copy-start | bytes 786436
  135.9 4.4 %copy-start.5 = (f32[17,17]{1,0:T(8,128)}, f32[17,17]{1,0:T(8,128)S(1)}, u32[]{:S(2)}) copy-start(f32[17,17]{1,0:T(8,128)S(1)} %psum.15) | copy-start | bytes 3472
Sparse Core Ops, SparseCore 0:
  10.6 39.0 all-reduce.1
where the time goes:
time: 202 us; the launch traced here: 201 us
  waiting for transfers between devices  52.8 us (26%)
  blocking collectives  39.4 us (20%)
  between operations  35.5 us (18%)
  other arithmetic  26.4 us (13%)
  local copies, waits for them, and re-layouts  23.1 us (11%)
  matrix products  18.9 us (9%)
  starting transfers between devices  4.76 us (2%)
    psum x1, blocking collectives, shards(): lax.psum(jnp.dot(vectors, vectors.T, precision=lax.Precision.HIGHEST), ('...  39.4 us
    psum x1, waiting for transfers between devices, shards(): summed = lax.psum(radial, 'event')  33.3 us
    ppermute x1, waiting for transfers between devices, with_halo(): lax.ppermute(head, axis, [((i + 1) % count, i) for i in range(count)])  19.6 us
    unnamed x21, local copies, waits for them, and re-layouts  13 us
    dot_general x8, other arithmetic, shards(): jnp.dot(products[PAIRS + pair], weights_now, precision=lax.Precision.HIGH...  10.6 us
    dot_general x8, other arithmetic, shards(): jnp.dot(products[pair], weights_now, precision=lax.Precision.HIGHEST)  9.85 us
    dot_general x1, matrix products, shards(): jnp.dot(vectors, vectors.T, precision=lax.Precision.HIGHEST)  8.77 us
    concatenate x1, local copies, waits for them, and re-layouts, shards(): jnp.concatenate([steps.reshape(PAIRS, -1), changes.reshape(PAIRS, -1), gr...  6.03 us
  transfers between devices with their start and end apart: 3, of which 2 were waited for; matrix products, arithmetic and copies ran while one was open for 4% of the time, Pallas kernels for 0%

commit v1 on v0

--- a/solution.py
+++ b/solution.py
@@ -66,7 +66,7 @@
         [steps.reshape(PAIRS, -1), changes.reshape(PAIRS, -1), gradient.reshape(1, -1)], axis=0
     )
     products = lax.psum(
-        jnp.dot(vectors, vectors.T, precision=lax.Precision.HIGHEST), ("cuts", "event")
+        lax.psum(jnp.dot(vectors, vectors.T, precision=lax.Precision.HIGHEST), "event"), "cuts"
     )
     curvs = jnp.diagonal(products[:PAIRS, PAIRS : 2 * PAIRS])
     inverse = 1.0 / curvs

time: 202 us -> 209 us (1.035)
  blocking collectives: 39.4 us -> 46.6 us
    psum x1 -> x2, blocking collectives: 39.4 us -> 46.6 us  [the longest x1 36.4 us: shards(): lax.psum(lax.psum(jnp.dot(vectors, vectors.T, precision=lax.Precision.HIG...]
where the time goes in v1:
time: 209 us; the launch traced here: 208 us
  waiting for transfers between devices  52.8 us (25%)
  blocking collectives  46.6 us (22%)
  between operations  35.5 us (17%)
  other arithmetic  26.4 us (13%)
  local copies, waits for them, and re-layouts  23.1 us (11%)
  matrix products  18.9 us (9%)
  starting transfers between devices  4.76 us (2%)
    psum x1, blocking collectives, shards(): lax.psum(lax.psum(jnp.dot(vectors, vectors.T, precision=lax.Precision.HIG...  36.4 us
    psum x1, waiting for transfers between devices, shards(): summed = lax.psum(radial, 'event')  33.3 us
    ppermute x1, waiting for transfers between devices, with_halo(): lax.ppermute(head, axis, [((i + 1) % count, i) for i in range(count)])  19.6 us
    unnamed x21, local copies, waits for them, and re-layouts  13 us
    dot_general x8, other arithmetic, shards(): jnp.dot(products[PAIRS + pair], weights_now, precision=lax.Precision.HIGH...  10.6 us
    psum x1, blocking collectives, shards(): lax.psum(jnp.dot(vectors, vectors.T, precision=lax.Precision.HIGHEST), 'e...  10.1 us
    dot_general x8, other arithmetic, shards(): jnp.dot(products[pair], weights_now, precision=lax.Precision.HIGHEST)  9.85 us
    dot_general x1, matrix products, shards(): jnp.dot(vectors, vectors.T, precision=lax.Precision.HIGHEST)  8.77 us
  transfers between devices with their start and end apart: 3, of which 2 were waited for; matrix products, arithmetic and copies ran while one was open for 4% of the time, Pallas kernels for 0%

profile of v1, /device:TPU:0, one launch (start us, length us, event | category | flops | bytes accessed | tf_op | source)
XLA Modules:
  0.0 208.0 jit_solution(7003556124055098034)
XLA Ops:
  7.4 1.0 copy-done
  8.4 2.0 fusion.11
  10.5 1.2 copy.40
  11.7 1.5 constant_dynamic-update-slice_fusion.1
  13.2 0.4 mul.113
  13.6 2.6 %copy.41 = f32[1,8,256,256]{3,1,2,0:T(8,128)} copy(f32[1,8,256,256]{3,2,1,0:T(8,128)S(1)} %bitcast.165) | data formatting | bytes 4194304
  16.2 0.2 fusion.28
  16.4 33.3 %all-reduce.2.cloned.1.call-done = f32[1024,256]{1,0:T(8,128)} async-done(((f32[1024,256]{1,0:T(8,128)}), f32[1024,256]{1,0:T(8,128)}) %all-reduce.2.cloned.1.call-update) | async-done | bytes 1048592 | tf_op jit(solution)/shard_map/psum | solution.py:60
  49.6 2.5 %fusion.25 = f32[1024,256]{1,0:T(8,128)S(1)} fusion(f32[1024,256]{1,0:T(8,128)} %all-reduce.2.cloned.1.call-done, f32[256]{0:T(256)S(1)} %fusion.28), kind=kOutput, calls=%fused_computation.48 | convolution fusion | flops 805634048 | bytes 2098176 | tf_op jit(solution)/shard_map/dot_general | solution.py:42
  52.1 0.9 fusion.74
  53.0 1.5 collective-permute-start
  54.5 3.2 %collective-permute-start.1 = (f32[4,128,256]{2,1,0:T(8,128)}, f32[4,128,256]{2,1,0:T(8,128)S(1)}, u32[]{:S(2)}, u32[]{:S(2)}) collective-permute-start(f32[4,128,256]{2,1,0:T(8,128)} %bitcast.6), channel_id=1, source_target_pairs={{4,0},{8,4},{12,8},{16,12},{20,16},{24,20},{28,24},{0,28},{5,1},{9... | collective-permute-start | bytes 1572872 | tf_op jit(solution)/shard_map/ppermute | solution.py:20
  57.7 1.4 constant_dynamic-update-slice_fusion
  59.2 19.6 %collective-permute-done.1 = f32[4,128,256]{2,1,0:T(8,128)S(1)} collective-permute-done((f32[4,128,256]{2,1,0:T(8,128)}, f32[4,128,256]{2,1,0:T(8,128)S(1)}, u32[]{:S(2)}, u32[]{:S(2)}) %collective-permute-start.1) | collective-permute-done | bytes 524320 | tf_op jit(solution)/shard_map/ppermute | solution.py:20
  78.7 0.3 pad_slice_fusion.4
  79.1 2.1 %fusion.4 = (f32[8,128,256]{2,1,0:T(8,128)S(1)}, f32[8,128,256]{2,1,0:T(8,128)S(1)}, f32[8,128,256]{2,1,0:T(8,128)S(1)}, f32[8,128,256]{2,1,0:T(8,128)S(1)}, f32[8,128,256]{2,1,0:T(8,128)S(1)}) fusion(f32[8,128,256]{2,1,0:T(8,128)S(1)} %bitcast.161, f32[4,128,256]{2,1,0:T(8,128)} %collective-permute-done), kind=kLoop, calls=%fused_computation.17 | loop fusion | flops 2621440 | bytes 6815744 | tf_op jit(solution)/shard_map/add | solution.py:50
  81.2 0.2 fusion.17
  81.4 0.3 reshape.412
  81.7 6.0 %dynamic-update-slice.38 = f32[17,65536]{1,0:T(8,128)} dynamic-update-slice(f32[17,65536]{1,0:T(8,128)} %constant_dynamic-update-slice_fusion, f32[1,65536]{1,0:T(1,128)S(1)} %reshape.412, s32[]{} %constant.465, s32[]{} %constant.463) | dynamic-update-slice | bytes 524292 | tf_op jit(solution)/shard_map/concatenate | solution.py:65
  87.7 8.8 %fusion.76 = f32[17,17]{1,0:T(8,128)S(1)} fusion(f32[17,65536]{1,0:T(8,128)} %dynamic-update-slice.38), kind=kOutput, calls=%fused_computation.135 | convolution fusion | flops 227278848 | bytes 4457604 | tf_op jit(solution)/shard_map/dot_general | solution.py:69
  96.5 10.1 %psum.22 = f32[17,17]{1,0:T(8,128)S(1)} all-reduce(f32[17,17]{1,0:T(8,128)S(1)} %fusion.76), channel_id=1, replica_groups=mesh['cuts'=8,'event'=4] {'event'}, use_global_device_ids=true, to_apply=%region_3.0 | all-reduce | flops 289 | bytes 2312 | tf_op jit(solution)/shard_map/psum | solution.py:69
  106.6 36.4 %psum.23 = f32[17,17]{1,0:T(8,128)S(1)} all-reduce(f32[17,17]{1,0:T(8,128)S(1)} %psum.22), channel_id=1, replica_groups=mesh['cuts'=8,'event'=4] {'cuts'}, use_global_device_ids=true, to_apply=%region_4.0 | all-reduce | flops 289 | bytes 2312 | tf_op jit(solution)/shard_map/psum | solution.py:68
  143.2 0.6 gather_fusion
  143.8 0.6 slice.344
  144.4 0.6 slice.402
  144.9 0.7 fusion.75
  145.6 0.6 fusion.70
  147.5 1.3 fusion.68
  150.2 1.3 fusion.66
  152.8 0.2 constant_dynamic-update-slice_fusion.13
  153.0 1.3 fusion.64
  155.6 0.2 constant_dynamic-update-slice_fusion.12
  155.7 1.3 fusion.62
  158.4 1.3 fusion.60
  161.2 1.3 fusion.58
  163.9 1.3 fusion.56
  167.9 1.3 fusion.54
  170.4 1.3 fusion.52
  173.1 1.4 fusion.50
  175.9 1.4 fusion.48
  178.7 1.3 fusion.46
  181.4 1.3 fusion.44
  184.1 1.4 fusion.42
  186.9 1.3 fusion.40
  189.6 4.8 %copy.42 = f32[3,8,256,256]{3,2,1,0:T(8,128)S(1)} copy(f32[3,8,256,256]{3,1,2,0:T(8,128)} %bitcast.159) | data formatting | bytes 12582912
  194.4 0.4 slice.419
  194.8 5.6 %fusion = f32[1,8,32,256]{3,0,2,1:T(1,128)S(1)} fusion(f32[8,32,256,17]{2,1,0,3:T(8,128)S(1)} %bitcast.160, f32[17]{0:T(128)S(1)} %add_dynamic-update-slice_fusion), kind=kOutput, calls=%fused_computation.1 | convolution fusion | flops 13369344 | bytes 4718660 | tf_op jit(solution)/shard_map/dot_general | solution.py:87
  200.4 0.7 bitcast_negate_fusion
  (35 shorter events, 2.2 us)
Async XLA Ops:
  7.2 1.2 copy-start
  7.2 3.3 %copy-start.1 = (f32[8,8,32,256]{3,2,1,0:T(8,128)S(1)}, f32[8,8,32,256]{3,2,1,0:T(8,128)}, u32[]{:S(2)}) copy-start(f32[8,8,32,256]{3,2,1,0:T(8,128)} %param.38) | copy-start | bytes 6291460
  7.2 42.4 %all-reduce.2.cloned.1.call-start = ((), (), s32[]{:S(2)}) async-start(), calls=%async_computation | async-start | bytes 2097152 | tf_op jit(solution)/shard_map/psum | solution.py:60
  10.5 2.7 %copy-start.3 = (f32[8,8,32,256]{3,2,1,0:T(8,128)S(1)}, f32[8,8,32,256]{3,2,1,0:T(8,128)}, u32[]{:S(2)}) copy-start(f32[8,8,32,256]{3,2,1,0:T(8,128)} %param.39) | copy-start | bytes 6291460
  16.2 43.0 %copy-start.6 = (f32[17]{0:T(128)S(1)}, f32[17]{0:T(128)}, u32[]{:S(2)}) copy-start(f32[17]{0:T(128)} %constant.416.clone.1) | copy-start | bytes 208
  49.6 8.1 %copy-start.2 = (f32[1,8,256,256]{3,1,2,0:T(8,128)S(1)}, f32[1,8,256,256]{3,1,2,0:T(8,128)}, u32[]{:S(2)}) copy-start(f32[1,8,256,256]{3,1,2,0:T(8,128)} %copy.41) | copy-start | bytes 6291460
  53.0 26.0 %collective-permute-start = (f32[4,128,256]{2,1,0:T(8,128)S(1)}, f32[4,128,256]{2,1,0:T(8,128)}, u32[]{:S(2)}, u32[]{:S(2)}) collective-permute-start(f32[4,128,256]{2,1,0:T(8,128)S(1)} %bitcast.169), channel_id=1, source_target_pairs={{0,4},{4,8},{8,12},{12,16},{16,20},{20,24},{24,28},{28,0},{1,5},{5... | collective-permute-start | bytes 1572872 | tf_op jit(solution)/shard_map/ppermute | solution.py:18
  54.5 24.2 %collective-permute-start.1 = (f32[4,128,256]{2,1,0:T(8,128)}, f32[4,128,256]{2,1,0:T(8,128)S(1)}, u32[]{:S(2)}, u32[]{:S(2)}) collective-permute-start(f32[4,128,256]{2,1,0:T(8,128)} %bitcast.6), channel_id=1, source_target_pairs={{4,0},{8,4},{12,8},{16,12},{20,16},{24,20},{28,24},{0,28},{5,1},{9... | collective-permute-start | bytes 1572872 | tf_op jit(solution)/shard_map/ppermute | solution.py:20
  81.4 15.1 %copy-start.4 = (f32[8,32,256]{2,1,0:T(8,128)}, f32[8,32,256]{2,1,0:T(8,128)S(1)}, u32[]{:S(2)}) copy-start(f32[8,32,256]{2,1,0:T(8,128)S(1)} %fusion.17) | copy-start | bytes 786436
  143.1 4.4 %copy-start.5 = (f32[17,17]{1,0:T(8,128)}, f32[17,17]{1,0:T(8,128)S(1)}, u32[]{:S(2)}) copy-start(f32[17,17]{1,0:T(8,128)S(1)} %psum.23) | copy-start | bytes 3472
Sparse Core Ops, SparseCore 0:
  10.6 39.0 all-reduce.1
